TPU v7x, 32 devices: a whole 2x2x4 slice. The times are simulated.
32 devices in a mesh: tok: 8 (over y, x, core), layer: 4 (over z).
Axes of the slice: x: 2, y: 2, z: 4, core: 2. Of those that a mesh axis runs over, the one named last changes fastest.
Arguments:
- activations: bfloat16 [4, 896, 5120], P(None, ('tok', 'layer')), may hold values from -9 to 9
- pos_weight: bfloat16 [4, 48, 5120], P('layer', None, 'tok'), may hold values from -1 to 1
- depth_weight: bfloat16 [4, 128, 5120], P('layer', None, 'tok'), may hold values from -0.01953125 to 0.01953125
- tags: int32 [896], P(('tok', 'layer')), may hold values from 0 to 47
- depths: int32 [896], P(('tok', 'layer')), may hold values from 2 to 14
- counts: int32 [32], P(('tok', 'layer')), may hold values from 1 to 28, 560 in all
Outputs:
- pos_grad: float32 [4, 48, 5120], P('layer', None, 'tok')
- depth_grad: float32 [4, 128, 5120], P('layer', None, 'tok')
Inputs may be any that keep to these rules, and one draw needn't show every extreme that they name: counts[d] is the number of live slots among device d's 28 slots, which are its first ones; the largest count equals 28.
All inputs are finite; a program needn't handle non-finite values.
Results may differ from a plain program's by a relative error of at most 0.0042.
Values may be sent and summed in bfloat16 or wider, within the bound.
No kernel may reach another device: no remote copies, remote signals or barrier semaphores. Data moves between devices by JAX's collectives and lax.ppermute only.
A program may use at most 64 MiB of HBM per device.

v0:
```python
import jax
import jax.numpy as jnp
from jax import lax
from jax.sharding import PartitionSpec as P


def contract(left, right):
    return lax.dot_general(
        left, right, (((1,), (1,)), ((), ())), preferred_element_type=jnp.float32
    )


def local(activations, pos_weight, depth_weight, tags, depths, counts):
    tag_count = pos_weight.shape[1]
    slots_each = tags.shape[0]
    owned_rows = lax.all_to_all(activations, "layer", split_axis=0, concat_axis=1, tiled=True)[0]
    row_count = owned_rows.shape[0]
    pos_full, depth_full = (
        lax.all_gather(pos_weight, "tok", axis=2, tiled=True),
        lax.all_gather(depth_weight, "tok", axis=2, tiled=True),
    )
    logits = contract(owned_rows, pos_full[0])
    hidden = contract(owned_rows, depth_full[0])
    tag_rows, depth_rows, block_counts = (
        lax.all_gather(tags, "layer", axis=0, tiled=True),
        lax.all_gather(depths, "layer", axis=0, tiled=True),
        lax.all_gather(counts, "layer", axis=0, tiled=True),
    )
    row_count = owned_rows.shape[0]
    slot_index = jnp.arange(row_count, dtype=jnp.int32)
    position = slot_index % slots_each
    block_index = slot_index // slots_each
    source_index = jnp.arange(block_counts.shape[0], dtype=jnp.int32)
    match = block_index[:, None] == source_index[None, :]
    block_count = jnp.sum(jnp.where(match, block_counts[None, :], 0), axis=1)
    live = position < block_count
    token_scale = jnp.where(live, 1.0 / block_count.astype(jnp.float32), jnp.float32(0.0))
    top = jnp.max(logits, axis=1, keepdims=True)
    expo = jnp.exp(logits - top)
    probabilities = expo / jnp.sum(expo, axis=1, keepdims=True)
    onehot = (tag_rows[:, None] == jnp.arange(tag_count, dtype=jnp.int32)[None, :]).astype(
        jnp.float32
    )
    g_pos = (probabilities - onehot) * token_scale[:, None]
    predicted = jnp.sum(hidden * hidden, axis=1)
    residual = predicted - depth_rows.astype(jnp.float32)
    g_depth = hidden * (residual * token_scale)[:, None]
    joined = jnp.concatenate([g_pos, g_depth], axis=1).astype(jnp.bfloat16)
    partial_value = lax.dot_general(
        joined, owned_rows, (((0,), (0,)), ((), ())), preferred_element_type=jnp.float32
    )
    summed = lax.psum_scatter(partial_value, "tok", scatter_dimension=1, tiled=True)
    return (summed[None, :tag_count], summed[None, tag_count:])


def solution(mesh):
    in_specs = (
        P(None, ("tok", "layer"), None),
        P("layer", None, "tok"),
        P("layer", None, "tok"),
        P(("tok", "layer")),
        P(("tok", "layer")),
        P(("tok", "layer")),
    )
    out_specs = (P("layer", None, "tok"), P("layer", None, "tok"))
    return jax.shard_map(local, mesh=mesh, in_specs=in_specs, out_specs=out_specs, check_vma=False)
```

profile of v0, /device:TPU:0, one launch (start us, length us, event | category | flops | bytes accessed | tf_op | source)
XLA Modules:
  0.0 121.3 jit_solution(3558480819830327647)
XLA Ops:
  7.2 0.0 all-gather.2.cloned.1.call-start
  7.2 0.7 all-gather.2.cloned.1.call-update
  7.9 2.7 %copy.13 = bf16[4,28,5120]{2,1,0:T(8,128)(2,1)} copy(bf16[4,28,5120]{2,0,1:T(4,128)(2,1)} %param.6) | data formatting | bytes 2293760 | tf_op args[0]
  10.6 6.5 %all-to-all-start = ((bf16[4,28,5120]{2,1,0:T(8,128)(2,1)}), bf16[4,28,5120]{2,1,0:T(8,128)(2,1)S(1)}, u32[]{:S(2)}, u32[]{:S(2)}) async-start(bf16[4,28,5120]{2,1,0:T(8,128)(2,1)} %copy.13), calls=%async_computation | async-start | bytes 2621440 | tf_op jit(solution)/shard_map/all_to_all | solution.py:16
  17.1 0.0 reduce-scatter.2.cloned.1.call-start
  17.8 0.6 dynamic-slice
  19.0 0.2 dynamic-update-slice.2
  19.3 0.2 dynamic-update-slice
  19.5 0.8 dynamic-update-slice.1
  20.3 28.4 %all-reduce.3 = (s32[4]{0:T(128)S(1)}, s32[112]{0:T(128)S(1)}, s32[112]{0:T(128)S(1)}) all-reduce(s32[4]{0:T(128)S(1)} %dynamic-update-slice.1, s32[112]{0:T(128)S(1)} %dynamic-update-slice.2, s32[112]{0:T(128)S(1)} %dynamic-update-slice), channel_id=1, replica_groups=mesh['tok'=8,'layer'=4] {'layer'}, use_global_device_ids=true, to_apply=%add.1 | all-reduce | flops 228 | bytes 1824
  48.6 10.0 %all_gather.15 = bf16[1,48,5120]{2,1,0:T(8,128)(2,1)S(1)} all-gather(bf16[1,48,640]{2,1,0:T(8,128)(2,1)S(1)} %copy-done), channel_id=1, replica_groups=mesh['tok'=8,'layer'=4] {'tok'}, dimensions={2}, use_global_device_ids=true | all-gather | bytes 552960 | tf_op jit(solution)/shard_map/all_gather | solution.py:19
  58.6 0.1 select_reduce_fusion
  58.7 0.0 all-to-all-done
  58.7 0.3 squeeze.9
  59.0 0.5 fusion.10
  59.6 0.0 all-gather.2.cloned.1.call-done
  59.6 1.9 %multiply_reduce_fusion = (f32[112]{0:T(128)S(1)}, f32[112,128]{1,0:T(8,128)S(1)}) fusion(bf16[112,5120]{1,0:T(8,128)(2,1)S(1)} %squeeze.9, bf16[1,128,5120]{2,1,0:T(8,128)(2,1)} %all-gather.2.cloned.1.call-done), kind=kOutput, calls=%fused_computation.11 | convolution fusion | flops 146829200 | bytes 2515392 | tf_op jit(solution)/shard_map/dot_general | solution.py:8
  61.6 0.1 copy.14
  61.7 0.1 multiply_convert_fusion
  61.8 2.5 %fusion.4 = f32[176,5120]{1,0:T(8,128)} fusion(bf16[112,5120]{1,0:T(8,128)(2,1)S(1)} %squeeze.9, bf16[112,128]{1,0:T(8,128)(2,1)S(1)} %multiply_convert_fusion, bf16[112,48]{1,0:T(8,128)(2,1)S(1)} %copy.14), kind=kOutput, calls=%fused_computation.6 | convolution fusion | flops 201929728 | bytes 4790784 | tf_op jit(solution)/shard_map/dot_general | solution.py:49
  64.3 0.0 reduce-scatter.2.cloned.1.call-update
  64.3 46.9 %reduce-scatter.2.cloned.1.call-done = f32[176,640]{1,0:T(8,128)} async-done(((f32[176,5120]{1,0:T(8,128)}), f32[176,640]{1,0:T(8,128)}) %reduce-scatter.2.cloned.1.call-update) | async-done | bytes 450576 | tf_op jit(solution)/shard_map/reduce_scatter | solution.py:52
  111.2 1.6 %slice_bitcast_fusion.1 = f32[1,48,640]{2,1,0:T(8,128)} fusion(f32[176,640]{1,0:T(8,128)} %reduce-scatter.2.cloned.1.call-done), kind=kLoop, calls=%fused_computation.5 | loop fusion | bytes 245760 | tf_op jit(solution)/shard_map/broadcast_in_dim | solution.py:53
  112.8 1.7 %slice_bitcast_fusion = f32[1,128,640]{2,1,0:T(8,128)} fusion(f32[176,640]{1,0:T(8,128)} %reduce-scatter.2.cloned.1.call-done), kind=kLoop, calls=%fused_computation.4 | loop fusion | bytes 655360 | tf_op jit(solution)/shard_map/broadcast_in_dim | solution.py:53
  (15 shorter events, 0.1 us)
Async XLA Ops:
  7.2 52.4 %all-gather.2.cloned.1.call-start = ((), (), s32[]{:S(2)}) async-start(), calls=%async_computation.2 | async-start | bytes 1474560 | tf_op jit(solution)/shard_map/all_gather | solution.py:20
  10.6 7.2 %copy-start.3 = (u32[32]{0:T(128)S(1)}, u32[32]{0:T(128)}, u32[]{:S(2)}) copy-start(u32[32]{0:T(128)} %constant.35) | copy-start | bytes 388
  10.6 8.4 %copy-start.1 = (s32[28]{0:T(128)S(1)}, s32[28]{0:T(128)}, u32[]{:S(2)}) copy-start(s32[28]{0:T(128)} %param.10) | copy-start | bytes 340
  10.6 8.7 %copy-start.2 = (s32[28]{0:T(128)S(1)}, s32[28]{0:T(128)}, u32[]{:S(2)}) copy-start(s32[28]{0:T(128)} %param.9) | copy-start | bytes 340
  10.6 38.0 %copy-start = (bf16[1,48,640]{2,1,0:T(8,128)(2,1)S(1)}, bf16[1,48,640]{2,1,0:T(8,128)(2,1)}, u32[]{:S(2)}) copy-start(bf16[1,48,640]{2,1,0:T(8,128)(2,1)} %param.7) | copy-start | bytes 184324
  10.6 48.1 %all-to-all-start = ((bf16[4,28,5120]{2,1,0:T(8,128)(2,1)}), bf16[4,28,5120]{2,1,0:T(8,128)(2,1)S(1)}, u32[]{:S(2)}, u32[]{:S(2)}) async-start(bf16[4,28,5120]{2,1,0:T(8,128)(2,1)} %copy.13), calls=%async_computation | async-start | bytes 2621440 | tf_op jit(solution)/shard_map/all_to_all | solution.py:16
  17.1 94.1 %reduce-scatter.2.cloned.1.call-start = ((), (), s32[]{:S(2)}) async-start(), calls=%async_computation.3 | async-start | bytes 4055040 | tf_op jit(solution)/shard_map/reduce_scatter | solution.py:52
Sparse Core Ops, SparseCore 0:
  9.9 27.1 all-gather.1
  64.4 46.7 reduce-scatter.1
where the time goes:
time: 122 us; the launch traced here: 121 us
  waiting for transfers between devices  47.6 us (39%)
  blocking collectives  38.3 us (31%)
  between operations  15.4 us (13%)
  local copies, waits for them, and re-layouts  8.21 us (7%)
  starting transfers between devices  6.53 us (5%)
  matrix products  4.97 us (4%)
    reduce_scatter x1, waiting for transfers between devices, local(): lax.psum_scatter(partial_value, 'tok', scatter_dimension=1, tiled=True)  46.9 us
    unnamed x1, blocking collectives  28.4 us
    all_gather x1, blocking collectives, local(): lax.all_gather(pos_weight, 'tok', axis=2, tiled=True)  9.97 us
    all_to_all x1, starting transfers between devices, local(): lax.all_to_all(activations, 'layer', split_axis=0, concat_axis=1, tiled=T...  6.49 us
    unnamed x16, local copies, waits for them, and re-layouts  4.53 us
    broadcast_in_dim x2, local copies, waits for them, and re-layouts, local(): return (summed[None, :tag_count], summed[None, tag_count:])  3.27 us
    dot_general x1, matrix products, local(): lax.dot_general(joined, owned_rows, (((0,), (0,)), ((), ())), preferred_e...  2.5 us
    dot_general x2, matrix products, contract(): lax.dot_general(left, right, (((1,), (1,)), ((), ())), preferred_element_...  2.47 us
  transfers between devices with their start and end apart: 3, of which 1 were waited for; matrix products, arithmetic and copies ran while one was open for 5% of the time, Pallas kernels for 0%

commit v1 on v0

--- a/solution.py
+++ b/solution.py
@@ -1,7 +1,17 @@
+import functools
 import jax
 import jax.numpy as jnp
 from jax import lax
 from jax.sharding import PartitionSpec as P
+
+
+def tell_cards(x_local, named_axis):
+    formed = lax.all_gather(x_local, named_axis)
+    big = jnp.concatenate(formed, 2)
+    return big
+
+
+unit_put = functools.partial(tell_cards, named_axis="tok")
 
 
 def contract(left, right):
@@ -16,7 +26,7 @@
     owned_rows = lax.all_to_all(activations, "layer", split_axis=0, concat_axis=1, tiled=True)[0]
     row_count = owned_rows.shape[0]
     pos_full, depth_full = (
-        lax.all_gather(pos_weight, "tok", axis=2, tiled=True),
+        unit_put(pos_weight),
         lax.all_gather(depth_weight, "tok", axis=2, tiled=True),
     )
     logits = contract(owned_rows, pos_full[0])

time: 122 us -> 122 us (level)
    unnamed x16 -> x17, local copies, waits for them, and re-layouts: 4.53 us -> 4.57 us
where the time goes in v1:
time: 122 us; the launch traced here: 121 us
  waiting for transfers between devices  47.6 us (39%)
  blocking collectives  38.2 us (31%)
  between operations  15.4 us (13%)
  local copies, waits for them, and re-layouts  8.25 us (7%)
  starting transfers between devices  6.53 us (5%)
  matrix products  4.97 us (4%)
    reduce_scatter x1, waiting for transfers between devices, local(): lax.psum_scatter(partial_value, 'tok', scatter_dimension=1, tiled=True)  46.9 us
    unnamed x1, blocking collectives  28.4 us
    all_gather x1, blocking collectives, tell_cards(): formed = lax.all_gather(x_local, named_axis)  9.84 us
    all_to_all x1, starting transfers between devices, local(): lax.all_to_all(activations, 'layer', split_axis=0, concat_axis=1, tiled=T...  6.49 us
    unnamed x17, local copies, waits for them, and re-layouts  4.57 us
    broadcast_in_dim x2, local copies, waits for them, and re-layouts, local(): return (summed[None, :tag_count], summed[None, tag_count:])  3.27 us
    dot_general x1, matrix products, local(): lax.dot_general(joined, owned_rows, (((0,), (0,)), ((), ())), preferred_e...  2.49 us
    dot_general x2, matrix products, contract(): lax.dot_general(left, right, (((1,), (1,)), ((), ())), preferred_element_...  2.47 us
  transfers between devices with their start and end apart: 3, of which 1 were waited for; matrix products, arithmetic and copies ran while one was open for 5% of the time, Pallas kernels for 0%

profile of v1, /device:TPU:0, one launch (start us, length us, event | category | flops | bytes accessed | tf_op | source)
XLA Modules:
  0.0 121.2 jit_solution(9883093201118089357)
XLA Ops:
  7.2 0.0 all-gather.3.cloned.1.call-start
  7.2 0.7 all-gather.3.cloned.1.call-update
  7.9 2.7 %copy.15 = bf16[4,28,5120]{2,1,0:T(8,128)(2,1)} copy(bf16[4,28,5120]{2,0,1:T(4,128)(2,1)} %param.6) | data formatting | bytes 2293760 | tf_op args[0]
  10.6 6.5 %all-to-all-start = ((bf16[4,28,5120]{2,1,0:T(8,128)(2,1)}), bf16[4,28,5120]{2,1,0:T(8,128)(2,1)S(1)}, u32[]{:S(2)}, u32[]{:S(2)}) async-start(bf16[4,28,5120]{2,1,0:T(8,128)(2,1)} %copy.15), calls=%async_computation | async-start | bytes 2621440 | tf_op jit(solution)/shard_map/all_to_all | solution.py:26
  17.1 0.0 reduce-scatter.2.cloned.1.call-start
  17.8 0.6 dynamic-slice
  19.0 0.2 dynamic-update-slice.2
  19.3 0.2 dynamic-update-slice
  19.5 0.8 dynamic-update-slice.1
  20.3 28.4 %all-reduce.3 = (s32[4]{0:T(128)S(1)}, s32[112]{0:T(128)S(1)}, s32[112]{0:T(128)S(1)}) all-reduce(s32[4]{0:T(128)S(1)} %dynamic-update-slice.1, s32[112]{0:T(128)S(1)} %dynamic-update-slice.2, s32[112]{0:T(128)S(1)} %dynamic-update-slice), channel_id=1, replica_groups=mesh['tok'=8,'layer'=4] {'layer'}, use_global_device_ids=true, to_apply=%add.1 | all-reduce | flops 228 | bytes 1824
  48.6 9.8 %all-gather = bf16[8,48,640]{2,1,0:T(8,128)(2,1)S(1)} all-gather(bf16[1,48,640]{2,1,0:T(8,128)(2,1)S(1)} %copy-done), channel_id=2, replica_groups=mesh['tok'=8,'layer'=4] {'tok'}, dimensions={0}, use_global_device_ids=true | all-gather | bytes 552960 | tf_op jit(solution)/shard_map/all_gather | solution.py:9
  58.5 0.1 select_reduce_fusion
  58.6 0.0 all-to-all-done
  58.6 0.3 squeeze.6
  58.9 0.5 fusion.8
  59.5 0.0 all-gather.3.cloned.1.call-done
  59.5 1.9 %multiply_reduce_fusion = (f32[112]{0:T(128)S(1)}, f32[112,128]{1,0:T(8,128)S(1)}) fusion(bf16[112,5120]{1,0:T(8,128)(2,1)S(1)} %squeeze.6, bf16[1,128,5120]{2,1,0:T(8,128)(2,1)} %all-gather.3.cloned.1.call-done), kind=kOutput, calls=%fused_computation.9 | convolution fusion | flops 146829200 | bytes 2515392 | tf_op jit(solution)/shard_map/dot_general | solution.py:18
  61.5 0.1 copy.17
  61.6 0.1 multiply_convert_fusion
  61.7 2.5 %fusion.2 = f32[176,5120]{1,0:T(8,128)} fusion(bf16[112,5120]{1,0:T(8,128)(2,1)S(1)} %squeeze.6, bf16[112,128]{1,0:T(8,128)(2,1)S(1)} %multiply_convert_fusion, bf16[112,48]{1,0:T(8,128)(2,1)S(1)} %copy.17), kind=kOutput, calls=%fused_computation.4 | convolution fusion | flops 201929728 | bytes 4790784 | tf_op jit(solution)/shard_map/dot_general | solution.py:59
  64.2 0.0 reduce-scatter.2.cloned.1.call-update
  64.2 46.9 %reduce-scatter.2.cloned.1.call-done = f32[176,640]{1,0:T(8,128)} async-done(((f32[176,5120]{1,0:T(8,128)}), f32[176,640]{1,0:T(8,128)}) %reduce-scatter.2.cloned.1.call-update) | async-done | bytes 450576 | tf_op jit(solution)/shard_map/reduce_scatter | solution.py:62
  111.1 1.6 %slice_bitcast_fusion.1 = f32[1,48,640]{2,1,0:T(8,128)} fusion(f32[176,640]{1,0:T(8,128)} %reduce-scatter.2.cloned.1.call-done), kind=kLoop, calls=%fused_computation.3 | loop fusion | bytes 245760 | tf_op jit(solution)/shard_map/broadcast_in_dim | solution.py:63
  112.7 1.7 %slice_bitcast_fusion = f32[1,128,640]{2,1,0:T(8,128)} fusion(f32[176,640]{1,0:T(8,128)} %reduce-scatter.2.cloned.1.call-done), kind=kLoop, calls=%fused_computation.2 | loop fusion | bytes 655360 | tf_op jit(solution)/shard_map/broadcast_in_dim | solution.py:63
  (16 shorter events, 0.1 us)
Async XLA Ops:
  7.2 52.4 %all-gather.3.cloned.1.call-start = ((), (), s32[]{:S(2)}) async-start(), calls=%async_computation.2 | async-start | bytes 1474560 | tf_op jit(solution)/shard_map/all_gather | solution.py:30
  10.6 7.2 %copy-start.3 = (u32[32]{0:T(128)S(1)}, u32[32]{0:T(128)}, u32[]{:S(2)}) copy-start(u32[32]{0:T(128)} %constant.35) | copy-start | bytes 388
  10.6 8.4 %copy-start.1 = (s32[28]{0:T(128)S(1)}, s32[28]{0:T(128)}, u32[]{:S(2)}) copy-start(s32[28]{0:T(128)} %param.10) | copy-start | bytes 340
  10.6 8.7 %copy-start.2 = (s32[28]{0:T(128)S(1)}, s32[28]{0:T(128)}, u32[]{:S(2)}) copy-start(s32[28]{0:T(128)} %param.9) | copy-start | bytes 340
  10.6 38.0 %copy-start = (bf16[1,48,640]{2,1,0:T(8,128)(2,1)S(1)}, bf16[1,48,640]{2,1,0:T(8,128)(2,1)}, u32[]{:S(2)}) copy-start(bf16[1,48,640]{2,1,0:T(8,128)(2,1)} %param.7) | copy-start | bytes 184324
  10.6 48.0 %all-to-all-start = ((bf16[4,28,5120]{2,1,0:T(8,128)(2,1)}), bf16[4,28,5120]{2,1,0:T(8,128)(2,1)S(1)}, u32[]{:S(2)}, u32[]{:S(2)}) async-start(bf16[4,28,5120]{2,1,0:T(8,128)(2,1)} %copy.15), calls=%async_computation | async-start | bytes 2621440 | tf_op jit(solution)/shard_map/all_to_all | solution.py:26
  17.1 94.0 %reduce-scatter.2.cloned.1.call-start = ((), (), s32[]{:S(2)}) async-start(), calls=%async_computation.3 | async-start | bytes 4055040 | tf_op jit(solution)/shard_map/reduce_scatter | solution.py:62
Sparse Core Ops, SparseCore 0:
  9.9 27.1 all-gather.2
  64.4 46.7 reduce-scatter.1
